TPU v7x, 32 devices: a whole 2x2x4 slice. The times are simulated.
32 devices in a mesh: date: 16 (over z, y, x), pix: 2 (over core).
Axes of the slice: x: 2, y: 2, z: 4, core: 2. Of those that a mesh axis runs over, the one named last changes fastest.
Arguments:
- reflect: bfloat16 [64, 6, 16384], P('date', None, 'pix'), may hold values from -8 to 8
- cloud_free: int32 [64, 16384], P('date', 'pix'), may hold values from 0 to 1, as said below
- days: int32 [64], P('date'), may hold values from 1 to 2079, as said below
Outputs:
- median: float32 [6, 16384], P(None, 'pix')
- slope: float32 [6, 16384], P(None, 'pix')
Inputs may be any that keep to these rules, and one draw needn't show every extreme that they name: `cloud_free`: every pixel is clear on at least one of the first 32 dates and on at least one of the others; clear shares differ between tiles. `days`: strictly increasing.
All inputs are finite; a program needn't handle non-finite values.
Results may differ from a plain program's by a relative error of at most 0.0003.
Values may be sent and summed in bfloat16 or wider, within the bound.
A program may use at most 64 MiB of HBM per device.

v0:
```python
import jax
import jax.numpy as jnp
from jax import lax
from jax.sharding import PartitionSpec as P

ridge = 1.0
sentinel = 100.0


def count_ranks(carry, own, piece):

    def step(i, state):
        less, equal, count = state
        other = lax.dynamic_index_in_dim(piece, i, 0, keepdims=True).astype(jnp.float32)
        less = less + (other < own).astype(jnp.float32)
        equal = equal + (other == own).astype(jnp.float32)
        count = count + (other[0, 0] < 50.0).astype(jnp.float32)
        return (less, equal, count)

    return lax.fori_loop(0, piece.shape[0], step, carry)


def select_sums(values, valid, less, equal, count):
    lower = jnp.floor((count - 1.0) / 2.0)
    upper = jnp.floor(count / 2.0)
    low_pick = valid[:, None, :] * ((less <= lower) & (lower < less + equal)).astype(jnp.float32)
    high_pick = valid[:, None, :] * ((less <= upper) & (upper < less + equal)).astype(jnp.float32)
    return (
        jnp.sum(low_pick * values, 0),
        jnp.sum(low_pick, 0),
        jnp.sum(high_pick * values, 0),
        jnp.sum(high_pick, 0),
    )


def finish_median(low_num, low_den, high_num, high_den):
    return 0.5 * (low_num / jnp.maximum(low_den, 1.0) + high_num / jnp.maximum(high_den, 1.0))


def column_median(moved):
    column = moved.astype(jnp.float32)
    column_valid = (column[:, 0, :] < 50.0).astype(jnp.float32)
    zeros = jnp.zeros(column.shape, jnp.float32)
    start_carry = (zeros, zeros, jnp.zeros((column.shape[2],), jnp.float32))
    less, equal, count = count_ranks(start_carry, column, moved)
    low_num, low_den, high_num, high_den = select_sums(column, column_valid, less, equal, count)
    return (column, column_valid, finish_median(low_num, low_den, high_num, high_den))


def fit_slope(s_zero, s_one, s_two, s_y, s_ty):
    first = s_zero + ridge
    determinant = first * (s_two + ridge) - s_one * s_one
    return (first[None, :] * s_ty - s_one[None, :] * s_y) / determinant[None, :]


def local(reflect, cloud_free, days):
    values = reflect.astype(jnp.float32)
    valid = cloud_free.astype(jnp.float32)
    years = days.astype(jnp.float32) / 365.0
    csum = jnp.sum(values * valid[:, None, :], 2)
    cnt = jnp.sum(valid, 1)
    csum, cnt = lax.psum((csum, cnt), "pix")
    scene_mean = csum / jnp.maximum(cnt, 1.0)[:, None]
    marked = jnp.where(valid[:, None, :] > 0, values, sentinel).astype(jnp.bfloat16)
    shifted = values - scene_mean[:, :, None]
    weighted = valid[:, None, :] * shifted
    s_zero = jnp.sum(valid, 0)
    s_one = jnp.sum(years[:, None] * valid, 0)
    s_two = jnp.sum((years * years)[:, None] * valid, 0)
    s_y = jnp.sum(weighted, 0)
    s_ty = jnp.sum(years[:, None, None] * weighted, 0)
    moved = lax.all_to_all(marked, "date", split_axis=2, concat_axis=0, tiled=True)
    column, column_valid, part_median = column_median(moved)
    median = lax.all_gather(part_median, "date", axis=1, tiled=True)
    s_y, s_ty, s_zero, s_one, s_two = lax.psum((s_y, s_ty, s_zero, s_one, s_two), "date")
    slope = fit_slope(s_zero, s_one, s_two, s_y, s_ty)
    return (median, slope)


def solution(mesh):
    placed = (P("date", None, "pix"), P("date", "pix"), P("date"))
    return jax.shard_map(
        local,
        mesh=mesh,
        in_specs=placed,
        out_specs=(P(None, "pix"), P(None, "pix")),
        check_vma=False,
    )
```

profile of v0, /device:TPU:0, one launch (start us, length us, event | category | flops | bytes accessed | tf_op | source)
XLA Modules:
  0.0 414.7 jit_solution(17819752993265104546)
XLA Ops:
  7.9 1.8 convert_reduce_fusion.1
  9.7 0.9 convert_element_type.50
  10.7 1.0 broadcast_compare_fusion
  11.6 1.3 fusion.4
  12.9 2.6 all-reduce.2
  15.6 3.0 fusion.8
  18.6 8.5 %copy.37 = bf16[4,6,8192]{1,0,2:T(4,128)(2,1)} copy(bf16[4,6,8192]{2,0,1:T(4,128)(2,1)S(1)} %get-tuple-element.172) | data formatting | bytes 786432 | tf_op jit(solution)/shard_map/convert_element_type | solution.py:64
  27.2 14.3 %reshape.24 = bf16[16,2,6144]{2,1,0:T(2,128)(2,1)} reshape(bf16[8192,4,6]{2,1,0:T(4,128)(2,1)} %bitcast.17) | data formatting | bytes 786432
  41.5 8.2 %all-to-all-start = ((bf16[16,2,6144]{2,1,0:T(2,128)(2,1)}), bf16[16,2,6144]{2,1,0:T(2,128)(2,1)S(1)}, u32[]{:S(2)}, u32[]{:S(2)}) async-start(bf16[16,2,6144]{2,1,0:T(2,128)(2,1)} %reshape.24), calls=%async_computation | async-start | bytes 786432 | tf_op jit(solution)/shard_map/all_to_all | solution.py:72
  49.7 72.8 %all-reduce.6.cloned.1.call-done = (f32[8192]{0:T(1024)}, f32[8192]{0:T(1024)}, f32[8192]{0:T(1024)}) async-done(((f32[8192]{0:T(1024)}, f32[8192]{0:T(1024)}, f32[8192]{0:T(1024)}), (f32[8192]{0:T(1024)}, f32[8192]{0:T(1024)}, f32[8192]{0:T(1024)})) %all-reduce.6.cloned.1.call-update) | async-done | bytes 98320 | tf_op jit(solution)/shard_map/psum | solution.py:75
  122.5 0.8 broadcast_add_fusion
  123.4 114.3 %all-reduce.8.cloned.1.call-done = (f32[6,8192]{1,0:T(8,128)}, f32[6,8192]{1,0:T(8,128)}) async-done(((f32[6,8192]{1,0:T(8,128)}, f32[6,8192]{1,0:T(8,128)}), (f32[6,8192]{1,0:T(8,128)}, f32[6,8192]{1,0:T(8,128)})) %all-reduce.8.cloned.1.call-update) | async-done | bytes 393232 | tf_op jit(solution)/shard_map/psum | solution.py:75
  237.7 1.8 subtract_divide_fusion
  239.5 20.0 %reshape.25 = bf16[8192,4,6]{2,1,0:T(4,128)(2,1)} reshape(bf16[16,2,6144]{2,1,0:T(2,128)(2,1)S(1)} %all-to-all-done) | data formatting | bytes 786432
  259.5 12.9 %copy.38 = bf16[16,4,6,512]{3,2,1,0:T(8,128)(2,1)} copy(bf16[16,4,6,512]{2,1,3,0:T(4,128)(2,1)} %bitcast.18) | data formatting | bytes 786432 | tf_op jit(solution)/shard_map/all_to_all | solution.py:72
  272.3 1.2 bitcast_convert_fusion
  273.7 91.0 %while.18 = (s32[]{:T(128)}, f32[64,6,512]{2,1,0:T(8,128)S(1)}, f32[64,6,512]{2,1,0:T(8,128)S(1)}, f32[512]{0:T(512)S(1)}, bf16[64,6,512]{2,1,0:T(8,128)(2,1)}, ...) while((s32[]{:T(128)}, f32[64,6,512]{2,1,0:T(8,128)S(1)}, f32[64,6,512]{2,1,0:T(8,128)S(1)}, ...), condition=%wide.region_1.0_spmd.clone, body=%wide.region_0.0_spmd.clone.sunk | while | flops 1577987 | bytes 3985508 | solution.py:20
  273.7 0.7 dynamic-slice_convert_fusion.2
  275.1 0.7 dynamic-slice_convert_fusion.2
  276.5 0.7 dynamic-slice_convert_fusion.2
  277.9 0.7 dynamic-slice_convert_fusion.2
  279.4 0.7 dynamic-slice_convert_fusion.2
  280.8 0.7 dynamic-slice_convert_fusion.2
  282.2 0.7 dynamic-slice_convert_fusion.2
  283.6 0.7 dynamic-slice_convert_fusion.2
  289.3 0.7 dynamic-slice_convert_fusion.2
  290.7 0.7 dynamic-slice_convert_fusion.2
  292.2 0.7 dynamic-slice_convert_fusion.2
  293.6 0.7 dynamic-slice_convert_fusion.2
  295.0 0.7 dynamic-slice_convert_fusion.2
  365.1 1.6 fusion.1
  366.8 40.4 %all_gather.3 = f32[6,8192]{1,0:T(8,128)S(1)} all-gather(f32[6,512]{1,0:T(8,128)S(1)} %add_multiply_fusion), channel_id=1, replica_groups=mesh['date'=16,'pix'=2] {'date'}, dimensions={1}, use_global_device_ids=true | all-gather | bytes 208896 | tf_op jit(solution)/shard_map/all_gather | solution.py:74
  (260 shorter events, 82.1 us)
Async XLA Ops:
  7.2 115.4 %all-reduce.6.cloned.1.call-start = ((), (), s32[]{:S(2)}) async-start(), calls=%async_computation.1 | async-start | bytes 196608 | tf_op jit(solution)/shard_map/psum | solution.py:75
  9.7 228.0 %all-reduce.8.cloned.1.call-start = ((), (), s32[]{:S(2)}) async-start(), calls=%async_computation.2 | async-start | bytes 1048576 | tf_op jit(solution)/shard_map/psum | solution.py:75
  41.5 198.0 %all-to-all-start = ((bf16[16,2,6144]{2,1,0:T(2,128)(2,1)}), bf16[16,2,6144]{2,1,0:T(2,128)(2,1)S(1)}, u32[]{:S(2)}, u32[]{:S(2)}) async-start(bf16[16,2,6144]{2,1,0:T(2,128)(2,1)} %reshape.24), calls=%async_computation | async-start | bytes 786432 | tf_op jit(solution)/shard_map/all_to_all | solution.py:72
Sparse Core Ops, SparseCore 0:
  13.8 108.7 all-reduce.5
  128.3 109.3 all-reduce.7
where the time goes:
time: 419 us; the launch traced here: 415 us
  waiting for transfers between devices  187 us (45%)
  other arithmetic  104 us (25%)
  local copies, waits for them, and re-layouts  56.4 us (13%)
  blocking collectives  43 us (10%)
  between operations  14.1 us (3%)
  starting transfers between devices  8.26 us (2%)
    psum x2, waiting for transfers between devices, local(): lax.psum((s_y, s_ty, s_zero, s_one, s_two), 'date')  187 us
    convert_element_type x64, other arithmetic, step(): lax.dynamic_index_in_dim(piece, i, 0, keepdims=True).astype(jnp.float32)  45.1 us
    add x64, other arithmetic, step(): equal = equal + (other == own).astype(jnp.float32)  42.9 us
    all_gather x1, blocking collectives, local(): median = lax.all_gather(part_median, 'date', axis=1, tiled=True)  40.4 us
    unnamed x4, local copies, waits for them, and re-layouts  35 us
    all_to_all x1, local copies, waits for them, and re-layouts, local(): lax.all_to_all(marked, 'date', split_axis=2, concat_axis=0, tiled=True)  12.9 us
    convert_element_type x1, local copies, waits for them, and re-layouts, local(): jnp.where(valid[:, None, :] > 0, values, sentinel).astype(jnp.bfloat16)  8.54 us
  transfers between devices with their start and end apart: 3, of which 2 were waited for; matrix products, arithmetic and copies ran while one was open for 8% of the time, Pallas kernels for 0%

commit v1 on v0

--- a/solution.py
+++ b/solution.py
@@ -71,7 +71,12 @@
     s_ty = jnp.sum(years[:, None, None] * weighted, 0)
     moved = lax.all_to_all(marked, "date", split_axis=2, concat_axis=0, tiled=True)
     column, column_valid, part_median = column_median(moved)
-    median = lax.all_gather(part_median, "date", axis=1, tiled=True)
+    ring = [part_median]
+    for hop in range(15):
+        ring.append(lax.ppermute(ring[-1], "date", [(dev, (dev + 1) % 16) for dev in range(16)]))
+    median = jnp.roll(
+        jnp.concatenate(ring[::-1], axis=1), (lax.axis_index("date") + 1) * ring[0].shape[1], axis=1
+    )
     s_y, s_ty, s_zero, s_one, s_two = lax.psum((s_y, s_ty, s_zero, s_one, s_two), "date")
     slope = fit_slope(s_zero, s_one, s_two, s_y, s_ty)
     return (median, slope)

time: 419 us -> 312 us (0.74)
  waiting for transfers between devices: 187 us -> 120 us
  blocking collectives: 43 us -> 2.62 us
    psum x2, waiting for transfers between devices: 187 us -> 0.01 us  [local(): lax.psum((s_y, s_ty, s_zero, s_one, s_two), 'date')]
    ppermute x0 -> x15, waiting for transfers between devices: none -> 107 us  [local(): lax.ppermute(ring[-1], 'date', [(dev, (dev + 1) % 16) for dev in range(16)])]
    all_gather x1 -> x0, blocking collectives: 40.4 us -> none  [local(): median = lax.all_gather(part_median, 'date', axis=1, tiled=True)]
    all_to_all x1, waiting for transfers between devices: 0.01 us -> 11.4 us  [local(): lax.all_to_all(marked, 'date', split_axis=2, concat_axis=0, tiled=True)]
    unnamed x4 -> x34, local copies, waits for them, and re-layouts: 35 us -> 34.4 us
  transfers between devices with their start and end apart: 3 -> 18, of which waited for: 2 -> 16; matrix products, arithmetic and copies ran while one was open for 8% -> 42% of each run, Pallas kernels for 0% -> 0%
where the time goes in v1:
time: 312 us; the launch traced here: 308 us
  waiting for transfers between devices  120 us (38%)
  other arithmetic  104 us (33%)
  local copies, waits for them, and re-layouts  56.5 us (18%)
  between operations  14.4 us (5%)
  starting transfers between devices  8.91 us (3%)
    ppermute x15, waiting for transfers between devices, local(): lax.ppermute(ring[-1], 'date', [(dev, (dev + 1) % 16) for dev in range(16)])  107 us
    convert_element_type x64, other arithmetic, step(): lax.dynamic_index_in_dim(piece, i, 0, keepdims=True).astype(jnp.float32)  45.1 us
    add x64, other arithmetic, step(): equal = equal + (other == own).astype(jnp.float32)  42.9 us
    unnamed x34, local copies, waits for them, and re-layouts  34.4 us
    all_to_all x1, local copies, waits for them, and re-layouts, local(): lax.all_to_all(marked, 'date', split_axis=2, concat_axis=0, tiled=True)  12.9 us
    all_to_all x1, waiting for transfers between devices, local(): lax.all_to_all(marked, 'date', split_axis=2, concat_axis=0, tiled=True)  11.4 us
    convert_element_type x1, local copies, waits for them, and re-layouts, local(): jnp.where(valid[:, None, :] > 0, values, sentinel).astype(jnp.bfloat16)  8.5 us
    all_to_all x1, starting transfers between devices, local(): lax.all_to_all(marked, 'date', split_axis=2, concat_axis=0, tiled=True)  8.18 us
  transfers between devices with their start and end apart: 18, of which 16 were waited for; matrix products, arithmetic and copies ran while one was open for 42% of the time, Pallas kernels for 0%

profile of v1, /device:TPU:0, one launch (start us, length us, event | category | flops | bytes accessed | tf_op | source)
XLA Modules:
  0.0 308.0 jit_solution(6323147509458287741)
XLA Ops:
  7.2 0.9 convert_element_type.50
  8.1 1.0 broadcast_compare_fusion
  9.7 1.8 convert_reduce_fusion.1
  11.5 1.3 fusion.4
  12.8 2.6 all-reduce.2
  15.5 3.0 fusion.8
  18.5 8.5 %copy.37 = bf16[4,6,8192]{1,0,2:T(4,128)(2,1)} copy(bf16[4,6,8192]{2,0,1:T(4,128)(2,1)S(1)} %get-tuple-element.172) | data formatting | bytes 786432 | tf_op jit(solution)/shard_map/convert_element_type | solution.py:64
  27.0 14.3 %reshape.24 = bf16[16,2,6144]{2,1,0:T(2,128)(2,1)} reshape(bf16[8192,4,6]{2,1,0:T(4,128)(2,1)} %bitcast.17) | data formatting | bytes 786432
  41.3 8.2 %all-to-all-start = ((bf16[16,2,6144]{2,1,0:T(2,128)(2,1)}), bf16[16,2,6144]{2,1,0:T(2,128)(2,1)S(1)}, u32[]{:S(2)}, u32[]{:S(2)}) async-start(bf16[16,2,6144]{2,1,0:T(2,128)(2,1)} %reshape.24), calls=%async_computation | async-start | bytes 786432 | tf_op jit(solution)/shard_map/all_to_all | solution.py:72
  51.0 11.4 %all-to-all-done = bf16[16,2,6144]{2,1,0:T(2,128)(2,1)S(1)} async-done(((bf16[16,2,6144]{2,1,0:T(2,128)(2,1)}), bf16[16,2,6144]{2,1,0:T(2,128)(2,1)S(1)}, u32[]{:S(2)}, u32[]{:S(2)}) %all-to-all-start) | async-done | bytes 393248 | tf_op jit(solution)/shard_map/all_to_all | solution.py:72
  62.4 20.0 %reshape.25 = bf16[8192,4,6]{2,1,0:T(4,128)(2,1)} reshape(bf16[16,2,6144]{2,1,0:T(2,128)(2,1)S(1)} %all-to-all-done) | data formatting | bytes 786432
  82.4 12.9 %copy.38 = bf16[16,4,6,512]{3,2,1,0:T(8,128)(2,1)} copy(bf16[16,4,6,512]{2,1,3,0:T(4,128)(2,1)} %bitcast.18) | data formatting | bytes 786432 | tf_op jit(solution)/shard_map/all_to_all | solution.py:72
  95.3 1.2 bitcast_convert_fusion
  96.6 91.0 %while.18 = (s32[]{:T(128)}, f32[64,6,512]{2,1,0:T(8,128)S(1)}, f32[64,6,512]{2,1,0:T(8,128)S(1)}, f32[512]{0:T(512)S(1)}, bf16[64,6,512]{2,1,0:T(8,128)(2,1)}, ...) while((s32[]{:T(128)}, f32[64,6,512]{2,1,0:T(8,128)S(1)}, f32[64,6,512]{2,1,0:T(8,128)S(1)}, ...), condition=%wide.region_1.0_spmd.clone, body=%wide.region_0.0_spmd.clone.sunk | while | flops 1577987 | bytes 3985508 | solution.py:20
  188.1 1.6 fusion.1
  190.3 6.8 %collective-permute-done = f32[6,512]{1,0:T(8,128)S(1)} collective-permute-done((f32[6,512]{1,0:T(8,128)S(1)}, f32[6,512]{1,0:T(8,128)S(1)}, u32[]{:S(2)}, u32[]{:S(2)}) %collective-permute-start) | collective-permute-done | bytes 12320 | tf_op jit(solution)/shard_map/ppermute | solution.py:76
  197.1 7.3 %collective-permute-done.1 = f32[6,512]{1,0:T(8,128)S(1)} collective-permute-done((f32[6,512]{1,0:T(8,128)S(1)}, f32[6,512]{1,0:T(8,128)S(1)}, u32[]{:S(2)}, u32[]{:S(2)}) %collective-permute-start.1) | collective-permute-done | bytes 12320 | tf_op jit(solution)/shard_map/ppermute | solution.py:76
  204.5 7.4 %collective-permute-done.2 = f32[6,512]{1,0:T(8,128)S(1)} collective-permute-done((f32[6,512]{1,0:T(8,128)S(1)}, f32[6,512]{1,0:T(8,128)S(1)}, u32[]{:S(2)}, u32[]{:S(2)}) %collective-permute-start.2) | collective-permute-done | bytes 12320 | tf_op jit(solution)/shard_map/ppermute | solution.py:76
  211.8 7.3 %collective-permute-done.3 = f32[6,512]{1,0:T(8,128)S(1)} collective-permute-done((f32[6,512]{1,0:T(8,128)S(1)}, f32[6,512]{1,0:T(8,128)S(1)}, u32[]{:S(2)}, u32[]{:S(2)}) %collective-permute-start.3) | collective-permute-done | bytes 12320 | tf_op jit(solution)/shard_map/ppermute | solution.py:76
  219.2 7.3 %collective-permute-done.4 = f32[6,512]{1,0:T(8,128)S(1)} collective-permute-done((f32[6,512]{1,0:T(8,128)S(1)}, f32[6,512]{1,0:T(8,128)S(1)}, u32[]{:S(2)}, u32[]{:S(2)}) %collective-permute-start.4) | collective-permute-done | bytes 12320 | tf_op jit(solution)/shard_map/ppermute | solution.py:76
  226.5 7.4 %collective-permute-done.5 = f32[6,512]{1,0:T(8,128)S(1)} collective-permute-done((f32[6,512]{1,0:T(8,128)S(1)}, f32[6,512]{1,0:T(8,128)S(1)}, u32[]{:S(2)}, u32[]{:S(2)}) %collective-permute-start.5) | collective-permute-done | bytes 12320 | tf_op jit(solution)/shard_map/ppermute | solution.py:76
  233.9 7.3 %collective-permute-done.6 = f32[6,512]{1,0:T(8,128)S(1)} collective-permute-done((f32[6,512]{1,0:T(8,128)S(1)}, f32[6,512]{1,0:T(8,128)S(1)}, u32[]{:S(2)}, u32[]{:S(2)}) %collective-permute-start.6) | collective-permute-done | bytes 12320 | tf_op jit(solution)/shard_map/ppermute | solution.py:76
  241.2 7.3 %collective-permute-done.7 = f32[6,512]{1,0:T(8,128)S(1)} collective-permute-done((f32[6,512]{1,0:T(8,128)S(1)}, f32[6,512]{1,0:T(8,128)S(1)}, u32[]{:S(2)}, u32[]{:S(2)}) %collective-permute-start.7) | collective-permute-done | bytes 12320 | tf_op jit(solution)/shard_map/ppermute | solution.py:76
  248.6 7.4 %collective-permute-done.8 = f32[6,512]{1,0:T(8,128)S(1)} collective-permute-done((f32[6,512]{1,0:T(8,128)S(1)}, f32[6,512]{1,0:T(8,128)S(1)}, u32[]{:S(2)}, u32[]{:S(2)}) %collective-permute-start.8) | collective-permute-done | bytes 12320 | tf_op jit(solution)/shard_map/ppermute | solution.py:76
  255.9 7.3 %collective-permute-done.9 = f32[6,512]{1,0:T(8,128)S(1)} collective-permute-done((f32[6,512]{1,0:T(8,128)S(1)}, f32[6,512]{1,0:T(8,128)S(1)}, u32[]{:S(2)}, u32[]{:S(2)}) %collective-permute-start.9) | collective-permute-done | bytes 12320 | tf_op jit(solution)/shard_map/ppermute | solution.py:76
  263.3 7.4 %collective-permute-done.10 = f32[6,512]{1,0:T(8,128)S(1)} collective-permute-done((f32[6,512]{1,0:T(8,128)S(1)}, f32[6,512]{1,0:T(8,128)S(1)}, u32[]{:S(2)}, u32[]{:S(2)}) %collective-permute-start.10) | collective-permute-done | bytes 12320 | tf_op jit(solution)/shard_map/ppermute | solution.py:76
  270.7 7.3 %collective-permute-done.11 = f32[6,512]{1,0:T(8,128)S(1)} collective-permute-done((f32[6,512]{1,0:T(8,128)S(1)}, f32[6,512]{1,0:T(8,128)S(1)}, u32[]{:S(2)}, u32[]{:S(2)}) %collective-permute-start.11) | collective-permute-done | bytes 12320 | tf_op jit(solution)/shard_map/ppermute | solution.py:76
  278.0 7.3 %collective-permute-done.12 = f32[6,512]{1,0:T(8,128)S(1)} collective-permute-done((f32[6,512]{1,0:T(8,128)S(1)}, f32[6,512]{1,0:T(8,128)S(1)}, u32[]{:S(2)}, u32[]{:S(2)}) %collective-permute-start.12) | collective-permute-done | bytes 12320 | tf_op jit(solution)/shard_map/ppermute | solution.py:76
  285.4 0.8 broadcast_add_fusion
  286.2 6.5 %collective-permute-done.13 = f32[6,512]{1,0:T(8,128)S(1)} collective-permute-done((f32[6,512]{1,0:T(8,128)S(1)}, f32[6,512]{1,0:T(8,128)S(1)}, u32[]{:S(2)}, u32[]{:S(2)}) %collective-permute-start.13) | collective-permute-done | bytes 12320 | tf_op jit(solution)/shard_map/ppermute | solution.py:76
  292.7 1.8 subtract_divide_fusion
  294.5 5.5 %collective-permute-done.14 = f32[6,512]{1,0:T(8,128)S(1)} collective-permute-done((f32[6,512]{1,0:T(8,128)S(1)}, f32[6,512]{1,0:T(8,128)S(1)}, u32[]{:S(2)}, u32[]{:S(2)}) %collective-permute-start.14) | collective-permute-done | bytes 12320 | tf_op jit(solution)/shard_map/ppermute | solution.py:76
  (321 shorter events, 93.4 us)
Async XLA Ops:
  41.3 21.1 %all-to-all-start = ((bf16[16,2,6144]{2,1,0:T(2,128)(2,1)}), bf16[16,2,6144]{2,1,0:T(2,128)(2,1)S(1)}, u32[]{:S(2)}, u32[]{:S(2)}) async-start(bf16[16,2,6144]{2,1,0:T(2,128)(2,1)} %reshape.24), calls=%async_computation | async-start | bytes 786432 | tf_op jit(solution)/shard_map/all_to_all | solution.py:72
  49.5 235.9 %all-reduce.6.cloned.1.call-start = ((), (), s32[]{:S(2)}) async-start(), calls=%async_computation.1 | async-start | bytes 196608 | tf_op jit(solution)/shard_map/psum | solution.py:80
  50.2 242.5 %all-reduce.8.cloned.1.call-start = ((), (), s32[]{:S(2)}) async-start(), calls=%async_computation.2 | async-start | bytes 1048576 | tf_op jit(solution)/shard_map/psum | solution.py:80
  189.7 7.4 %collective-permute-start = (f32[6,512]{1,0:T(8,128)S(1)}, f32[6,512]{1,0:T(8,128)S(1)}, u32[]{:S(2)}, u32[]{:S(2)}) collective-permute-start(f32[6,512]{1,0:T(8,128)S(1)} %add_multiply_fusion), channel_id=1, source_target_pairs={{0,2},{2,4},{4,6},{6,8},{8,10},{10,12},{12,14},{14,16},{16,18},{18... | collective-permute-start | bytes 36872 | tf_op jit(solution)/shard_map/ppermute | solution.py:76
  197.1 7.3 %collective-permute-start.1 = (f32[6,512]{1,0:T(8,128)S(1)}, f32[6,512]{1,0:T(8,128)S(1)}, u32[]{:S(2)}, u32[]{:S(2)}) collective-permute-start(f32[6,512]{1,0:T(8,128)S(1)} %collective-permute-done), channel_id=1, source_target_pairs={{0,2},{2,4},{4,6},{6,8},{8,10},{10,12},{12,14},{14,16},{16,18},{18... | collective-permute-start | bytes 36872 | tf_op jit(solution)/shard_map/ppermute | solution.py:76
  204.5 7.4 %collective-permute-start.2 = (f32[6,512]{1,0:T(8,128)S(1)}, f32[6,512]{1,0:T(8,128)S(1)}, u32[]{:S(2)}, u32[]{:S(2)}) collective-permute-start(f32[6,512]{1,0:T(8,128)S(1)} %collective-permute-done.1), channel_id=1, source_target_pairs={{0,2},{2,4},{4,6},{6,8},{8,10},{10,12},{12,14},{14,16},{16,18},{18... | collective-permute-start | bytes 36872 | tf_op jit(solution)/shard_map/ppermute | solution.py:76
  211.8 7.3 %collective-permute-start.3 = (f32[6,512]{1,0:T(8,128)S(1)}, f32[6,512]{1,0:T(8,128)S(1)}, u32[]{:S(2)}, u32[]{:S(2)}) collective-permute-start(f32[6,512]{1,0:T(8,128)S(1)} %collective-permute-done.2), channel_id=1, source_target_pairs={{0,2},{2,4},{4,6},{6,8},{8,10},{10,12},{12,14},{14,16},{16,18},{18... | collective-permute-start | bytes 36872 | tf_op jit(solution)/shard_map/ppermute | solution.py:76
  219.2 7.3 %collective-permute-start.4 = (f32[6,512]{1,0:T(8,128)S(1)}, f32[6,512]{1,0:T(8,128)S(1)}, u32[]{:S(2)}, u32[]{:S(2)}) collective-permute-start(f32[6,512]{1,0:T(8,128)S(1)} %collective-permute-done.3), channel_id=1, source_target_pairs={{0,2},{2,4},{4,6},{6,8},{8,10},{10,12},{12,14},{14,16},{16,18},{18... | collective-permute-start | bytes 36872 | tf_op jit(solution)/shard_map/ppermute | solution.py:76
  226.5 7.4 %collective-permute-start.5 = (f32[6,512]{1,0:T(8,128)S(1)}, f32[6,512]{1,0:T(8,128)S(1)}, u32[]{:S(2)}, u32[]{:S(2)}) collective-permute-start(f32[6,512]{1,0:T(8,128)S(1)} %collective-permute-done.4), channel_id=1, source_target_pairs={{0,2},{2,4},{4,6},{6,8},{8,10},{10,12},{12,14},{14,16},{16,18},{18... | collective-permute-start | bytes 36872 | tf_op jit(solution)/shard_map/ppermute | solution.py:76
  233.9 7.3 %collective-permute-start.6 = (f32[6,512]{1,0:T(8,128)S(1)}, f32[6,512]{1,0:T(8,128)S(1)}, u32[]{:S(2)}, u32[]{:S(2)}) collective-permute-start(f32[6,512]{1,0:T(8,128)S(1)} %collective-permute-done.5), channel_id=1, source_target_pairs={{0,2},{2,4},{4,6},{6,8},{8,10},{10,12},{12,14},{14,16},{16,18},{18... | collective-permute-start | bytes 36872 | tf_op jit(solution)/shard_map/ppermute | solution.py:76
  241.2 7.3 %collective-permute-start.7 = (f32[6,512]{1,0:T(8,128)S(1)}, f32[6,512]{1,0:T(8,128)S(1)}, u32[]{:S(2)}, u32[]{:S(2)}) collective-permute-start(f32[6,512]{1,0:T(8,128)S(1)} %collective-permute-done.6), channel_id=1, source_target_pairs={{0,2},{2,4},{4,6},{6,8},{8,10},{10,12},{12,14},{14,16},{16,18},{18... | collective-permute-start | bytes 36872 | tf_op jit(solution)/shard_map/ppermute | solution.py:76
  248.6 7.4 %collective-permute-start.8 = (f32[6,512]{1,0:T(8,128)S(1)}, f32[6,512]{1,0:T(8,128)S(1)}, u32[]{:S(2)}, u32[]{:S(2)}) collective-permute-start(f32[6,512]{1,0:T(8,128)S(1)} %collective-permute-done.7), channel_id=1, source_target_pairs={{0,2},{2,4},{4,6},{6,8},{8,10},{10,12},{12,14},{14,16},{16,18},{18... | collective-permute-start | bytes 36872 | tf_op jit(solution)/shard_map/ppermute | solution.py:76
  255.9 7.3 %collective-permute-start.9 = (f32[6,512]{1,0:T(8,128)S(1)}, f32[6,512]{1,0:T(8,128)S(1)}, u32[]{:S(2)}, u32[]{:S(2)}) collective-permute-start(f32[6,512]{1,0:T(8,128)S(1)} %collective-permute-done.8), channel_id=1, source_target_pairs={{0,2},{2,4},{4,6},{6,8},{8,10},{10,12},{12,14},{14,16},{16,18},{18... | collective-permute-start | bytes 36872 | tf_op jit(solution)/shard_map/ppermute | solution.py:76
  263.3 7.4 %collective-permute-start.10 = (f32[6,512]{1,0:T(8,128)S(1)}, f32[6,512]{1,0:T(8,128)S(1)}, u32[]{:S(2)}, u32[]{:S(2)}) collective-permute-start(f32[6,512]{1,0:T(8,128)S(1)} %collective-permute-done.9), channel_id=1, source_target_pairs={{0,2},{2,4},{4,6},{6,8},{8,10},{10,12},{12,14},{14,16},{16,18},{18... | collective-permute-start | bytes 36872 | tf_op jit(solution)/shard_map/ppermute | solution.py:76
  270.7 7.3 %collective-permute-start.11 = (f32[6,512]{1,0:T(8,128)S(1)}, f32[6,512]{1,0:T(8,128)S(1)}, u32[]{:S(2)}, u32[]{:S(2)}) collective-permute-start(f32[6,512]{1,0:T(8,128)S(1)} %collective-permute-done.10), channel_id=1, source_target_pairs={{0,2},{2,4},{4,6},{6,8},{8,10},{10,12},{12,14},{14,16},{16,18},{18... | collective-permute-start | bytes 36872 | tf_op jit(solution)/shard_map/ppermute | solution.py:76
  278.0 7.3 %collective-permute-start.12 = (f32[6,512]{1,0:T(8,128)S(1)}, f32[6,512]{1,0:T(8,128)S(1)}, u32[]{:S(2)}, u32[]{:S(2)}) collective-permute-start(f32[6,512]{1,0:T(8,128)S(1)} %collective-permute-done.11), channel_id=1, source_target_pairs={{0,2},{2,4},{4,6},{6,8},{8,10},{10,12},{12,14},{14,16},{16,18},{18... | collective-permute-start | bytes 36872 | tf_op jit(solution)/shard_map/ppermute | solution.py:76
  285.4 7.3 %collective-permute-start.13 = (f32[6,512]{1,0:T(8,128)S(1)}, f32[6,512]{1,0:T(8,128)S(1)}, u32[]{:S(2)}, u32[]{:S(2)}) collective-permute-start(f32[6,512]{1,0:T(8,128)S(1)} %collective-permute-done.12), channel_id=1, source_target_pairs={{0,2},{2,4},{4,6},{6,8},{8,10},{10,12},{12,14},{14,16},{16,18},{18... | collective-permute-start | bytes 36872 | tf_op jit(solution)/shard_map/ppermute | solution.py:76
  292.7 7.3 %collective-permute-start.14 = (f32[6,512]{1,0:T(8,128)S(1)}, f32[6,512]{1,0:T(8,128)S(1)}, u32[]{:S(2)}, u32[]{:S(2)}) collective-permute-start(f32[6,512]{1,0:T(8,128)S(1)} %collective-permute-done.13), channel_id=1, source_target_pairs={{0,2},{2,4},{4,6},{6,8},{8,10},{10,12},{12,14},{14,16},{16,18},{18... | collective-permute-start | bytes 36872 | tf_op jit(solution)/shard_map/ppermute | solution.py:76
Sparse Core Ops, SparseCore 0:
  56.1 107.3 all-reduce.5
  169.2 109.3 all-reduce.7
